TPU v7x, 32 devices: a whole 2x2x4 slice. The times are simulated.
32 devices in a mesh: seq: 8 (over z, y), grp: 4 (over x, core).
Axes of the slice: x: 2, y: 2, z: 4, core: 2. Of those that a mesh axis runs over, the one named last changes fastest.
Arguments:
- frames: bfloat16 [16384, 1024], P(('seq', 'grp')), may hold values from -6 to 6
- ln1_gain: float32 [1024], replicated, may hold values from 0.1 to 1.9
- w_in: bfloat16 [1024, 2, 1024], P('seq', None, 'grp'), may hold values from -0.1875 to 0.1875
- w_dw: bfloat16 [31, 1024], replicated, may hold values from -1 to 1
- ln2_gain: float32 [1024], replicated, may hold values from 0.1 to 1.9
- ln2_bias: float32 [1024], replicated, may hold values from -3 to 3
- w_out: bfloat16 [1024, 1024], P('grp', 'seq'), may hold values from -0.1875 to 0.1875
- block_utt: int32 [128], replicated, may hold values from 0 to 31, as said below
- block_off: int32 [128], replicated, may hold values from 0 to 6, as said below
- lengths: int32 [32], replicated, may hold values from 1 to 896, as said below
Outputs:
- result: bfloat16 [16384, 1024], P(('seq', 'grp'))
Inputs may be any that keep to these rules, and one draw needn't show every extreme that they name: block_utt never falls along the blocks and names every utterance; each utterance is one run of 1 to 7 whole blocks, and some utterance has exactly 7. block_off counts the blocks of the run before a block, starting at 0. `lengths`: an utterance of n blocks has more than (n - 1) * 128 and at most n * 128 live frames.
All inputs are finite; a program needn't handle non-finite values.
Results may differ from a plain program's by a relative error of at most 0.0046.
Values may be sent and summed in bfloat16 or wider, within the bound.
A program may use at most 64 MiB of HBM per device.

v0:
```python
import jax
import jax.numpy as jnp
from jax import lax
from jax.sharding import PartitionSpec as P

D = 1024
KER = 31
BLK = 128
epsilon = 1e-05


def extended(block, sides, width):
    for axis, dim in sides:
        count = lax.axis_size(axis)
        forward = [(i, i + 1) for i in range(count - 1)]
        backward = [(target, source) for source, target in forward]
        low = lax.ppermute(
            lax.slice_in_dim(block, block.shape[dim] - width, None, axis=dim), axis, forward
        )
        high = lax.ppermute(lax.slice_in_dim(block, 0, width, axis=dim), axis, backward)
        block = jnp.concatenate([low, block, high], axis=dim)
    return block


def frame_keys(block_utt, block_off, lengths, first_row, row_count, margin):
    places = first_row - margin + jnp.arange(row_count + 2 * margin, dtype=jnp.int32)
    total_rows = block_utt.shape[0] * BLK
    inside = (places >= 0) & (places < total_rows)
    blocks = jnp.clip(places // BLK, 0, block_utt.shape[0] - 1)
    utterance = jnp.take(block_utt, blocks)
    position = jnp.take(block_off, blocks) * BLK + places % BLK
    living = inside & (position < jnp.take(lengths, utterance))
    return (jnp.where(living, utterance, -1), living[margin : margin + row_count])


def layer_norm(rows, gain):
    values = rows.astype(jnp.float32)
    average = jnp.mean(values, axis=1, keepdims=True)
    centered = values - average
    spread = jnp.mean(centered * centered, axis=1, keepdims=True)
    return (centered * lax.rsqrt(spread + epsilon) * gain).astype(jnp.bfloat16)


def gate_units(projected, living):
    half = projected.shape[1] // 2
    values = projected[:, :half] * jax.nn.sigmoid(projected[:, half:])
    return (values * living.astype(jnp.float32)[:, None]).astype(jnp.bfloat16)


def depthwise(widened, keys_wide, taps, row_count):
    margin = (taps.shape[0] - 1) // 2
    center = keys_wide[margin : margin + row_count]
    summed = jnp.zeros((row_count, widened.shape[1]), jnp.float32)
    for tap_index in range(taps.shape[0]):
        shifted = widened[tap_index : tap_index + row_count].astype(jnp.float32)
        same = (keys_wide[tap_index : tap_index + row_count] == center)[:, None]
        summed = summed + jnp.where(same, shifted, 0.0) * taps[tap_index].astype(jnp.float32)
    return summed


def finish(mixed, stat_sum, square_sum, width_total, gain, bias):
    average = stat_sum / width_total
    spread = square_sum / width_total - average * average
    normed = (mixed - average[:, None]) * lax.rsqrt(spread + epsilon)[:, None] * gain + bias
    return (normed * jax.nn.sigmoid(normed)).astype(jnp.bfloat16)


def project_rows(normed, row_count, column_count):

    def add_rows(total, weight_piece, start_row):
        piece_rows = weight_piece.shape[0]
        return jnp.dot(
            normed, weight_piece.reshape(piece_rows, -1), preferred_element_type=jnp.float32
        )

    return (add_rows, jnp.zeros((row_count, column_count), jnp.float32))


def per_device(
    frames, ln1_gain, w_in, w_dw, ln2_gain, ln2_bias, w_out, block_utt, block_off, lengths
):
    row_count = frames.shape[0]
    margin = (KER - 1) // 2
    own_first = lax.axis_index(("seq", "grp")) * row_count
    keys_wide, living = frame_keys(block_utt, block_off, lengths, own_first, row_count, margin)
    normed = layer_norm(frames, ln1_gain)
    w_in_rows, w_out_rows = (
        lax.all_gather(w_in, "grp", axis=2, tiled=True),
        lax.all_gather(w_out, "grp", axis=0, tiled=True),
    )
    add_rows, empty = project_rows(normed, row_count, 2 * D)
    projected = add_rows(empty, lax.all_gather(w_in_rows, "seq", axis=0, tiled=True), jnp.int32(0))
    gated = gate_units(projected, living)
    widened = extended(gated, ((("seq", "grp"), 0),), margin)
    mixed = depthwise(widened, keys_wide, w_dw, row_count)
    act = finish(
        mixed, jnp.sum(mixed, axis=1), jnp.sum(mixed * mixed, axis=1), float(D), ln2_gain, ln2_bias
    )
    output = jnp.dot(
        act,
        lax.all_gather(w_out_rows, "seq", axis=1, tiled=True),
        preferred_element_type=jnp.float32,
    )
    alive = living.astype(jnp.float32)[:, None]
    return (frames.astype(jnp.float32) + output * alive).astype(jnp.bfloat16)


def solution(mesh):
    return jax.shard_map(
        per_device,
        mesh=mesh,
        in_specs=(
            P(("seq", "grp"), None),
            P(),
            P("seq", None, "grp"),
            P(),
            P(),
            P(),
            P("grp", "seq"),
            P(),
            P(),
            P(),
        ),
        out_specs=P(("seq", "grp"), None),
        check_vma=False,
    )
```

profile of v0, /device:TPU:0, one launch (start us, length us, event | category | flops | bytes accessed | tf_op | source)
XLA Modules:
  0.0 152.2 jit_solution(5140980709808963621)
XLA Ops:
  6.5 0.0 copy-start
  6.5 0.0 all-gather.3.cloned.1.call-start
  6.5 10.5 %all_gather.12 = bf16[128,2,1024]{2,1,0:T(2,128)(2,1)} all-gather(bf16[128,2,256]{2,1,0:T(2,128)(2,1)} %param.14), channel_id=1, replica_groups=mesh['seq'=8,'grp'=4] {'grp'}, dimensions={2}, use_global_device_ids=true | all-gather | bytes 655360 | tf_op jit(solution)/shard_map/all_gather | solution.py:88
  17.0 0.0 all-gather.3.cloned.1.call-update
  17.0 0.0 all-gather.5.cloned.1.call-start
  17.1 6.5 %all_gather.14 = bf16[1024,128]{1,0:T(8,128)(2,1)} all-gather(bf16[256,128]{1,0:T(8,128)(2,1)} %param.18), channel_id=1, replica_groups=mesh['seq'=8,'grp'=4] {'grp'}, dimensions={0}, use_global_device_ids=true | all-gather | bytes 327680 | tf_op jit(solution)/shard_map/all_gather | solution.py:89
  23.6 0.0 all-gather.5.cloned.1.call-update
  23.6 2.1 %fusion.67 = (s32[1]{0:T(128)}, s32[1]{0:T(128)}, s32[1]{0:T(128)}, s32[1]{0:T(128)}, s32[1]{0:T(128)}, /*index=5*/s32[1]{0:T(128)}, s32[1]{0:T(128)}, s32[1]{0:...) fusion(s32[32]{0:T(128)} %param.21), kind=kLoop, calls=%fused_computation.200 | loop fusion | bytes 152 | tf_op jit(solution)/shard_map/jit(_take)/gather | solution.py:32
  25.7 1.8 %fusion.68 = (s32[1]{0:T(128)}, s32[1]{0:T(128)}, s32[1]{0:T(128)}, s32[1]{0:T(128)}, s32[1]{0:T(128)}, /*index=5*/s32[1]{0:T(128)}, s32[1]{0:T(128)}, s32[1]{0:...) fusion(s32[32]{0:T(128)} %param.21), kind=kLoop, calls=%fused_computation.201 | loop fusion | bytes 104 | tf_op jit(solution)/shard_map/jit(_take)/gather | solution.py:32
  27.6 0.0 copy-done
  27.6 0.0 copy-start.1
  27.6 3.8 %gather_fusion = s32[542]{0:T(1024)S(1)} fusion(s32[128]{0:T(128)S(1)} %copy-done, s32[1024]{0:T(1024)S(1)} %pad_clamp_fusion), kind=kCustom, calls=%fused_computation.clone | custom fusion | bytes 6504 | tf_op jit(solution)/shard_map/jit(_take)/gather | solution.py:31
  31.4 0.0 copy-done.1
  31.4 0.0 copy-start.3
  31.4 0.0 copy-start.2
  31.4 3.8 %gather_fusion.1 = s32[542]{0:T(1024)S(1)} fusion(s32[128]{0:T(128)S(1)} %copy-done.1, s32[1024]{0:T(1024)S(1)} %pad_clamp_fusion), kind=kCustom, calls=%fused_computation.1.clone | custom fusion | bytes 6504 | tf_op jit(solution)/shard_map/jit(_take)/gather | solution.py:30
  35.3 20.1 %fusion.62 = (s32[542]{0:T(1024)S(1)}, pred[542]{0:T(1024)(128)(4,1)S(1)}) fusion(s32[542]{0:T(1024)S(1)} %gather_fusion.1, s32[]{:T(128)S(6)} %sub.32, s32[]{:T(128)} %bitcast.31, s32[]{:T(128)} %bitcast.30, s32[]{:T(128)} %bitcast.29, s32[]{:T(128)} %bitcast.28, s32[]{:T(128)} %bitcast.27, s32[]{:T(128)} %bitcast.26, s32[]{:T(128)} %bitcast.25, ...), kind=kLoop, calls=%fused_computation.161 | loop fusion | flops 57452 | bytes 7178 | tf_op jit(solution)/shard_map/jit(_where)/select_n | solution.py:33
  55.4 0.1 slice_compare_fusion.29
  55.5 0.1 slice_compare_fusion.28
  55.6 0.1 slice_compare_fusion.27
  55.7 0.0 copy-done.3
  55.7 0.1 slice_convert_fusion.30
  55.8 0.1 slice_convert_fusion.31
  55.9 0.0 copy-done.2
  55.9 0.2 convert_reduce_fusion
  56.1 0.4 fusion.2
  56.5 33.8 %all-gather.3.cloned.1.call-done = bf16[1024,2,1024]{2,1,0:T(2,128)(2,1)} async-done(((bf16[128,2,1024]{2,1,0:T(2,128)(2,1)}), bf16[1024,2,1024]{2,1,0:T(2,128)(2,1)}) %all-gather.3.cloned.1.call-update) | async-done | bytes 4194320 | tf_op jit(solution)/shard_map/all_gather | solution.py:92
  90.3 0.0 copy-start.4
  90.3 3.6 %copy.11 = bf16[128,8,2,1024]{3,1,2,0:T(8,128)(2,1)S(1)} copy(bf16[128,8,2,1024]{3,2,1,0:T(2,128)(2,1)} %bitcast.67) | data formatting | bytes 8388608
  94.0 0.0 copy-done.4
  94.0 2.5 %fusion.12 = f32[512,2048]{1,0:T(8,128)S(1)} fusion(bf16[1024,2048]{1,0:T(8,128)(2,1)S(1)} %bitcast.68, bf16[512,1024]{1,0:T(8,128)(2,1)S(1)} %copy-done.2, f32[1024]{0:T(1024)S(1)} %copy-done.4, f32[512]{0:T(512)S(1)} %add_rsqrt_fusion.1, f32[512]{0:T(512)S(1)} %broadcast_multiply_fusion.1), kind=kOutput, calls=%fused_computation.49 | convolution fusion | flops 2150105088 | bytes 9445376 | tf_op jit(solution)/shard_map/dot_general | solution.py:72
  96.5 0.6 fusion.11
  97.0 0.0 copy-start.5
  97.1 0.0 copy-start.6
  97.1 1.3 collective-permute-start
  98.4 1.5 collective-permute-start.1
  99.9 0.1 slice_compare_fusion.26
  99.9 0.0 collective-permute-done
  99.9 3.3 %collective-permute-done.1 = bf16[15,1024]{1,0:T(8,128)(2,1)S(1)} collective-permute-done((bf16[15,1024]{1,0:T(8,128)(2,1)S(1)}, bf16[15,1024]{1,0:T(8,128)(2,1)S(1)}, u32[]{:S(2)}, u32[]{:S(2)}) %collective-permute-start.1) | collective-permute-done | bytes 30752 | tf_op jit(solution)/shard_map/ppermute | solution.py:20
  103.2 19.4 %fusion.64 = (f32[512]{0:T(512)S(1)}, f32[512]{0:T(512)S(1)}, f32[512,1024]{1,0:T(8,128)S(1)}) fusion(f32[1024]{0:T(1024)S(1)} %bitcast.98, bf16[15,1024]{1,0:T(8,128)(2,1)S(1)} %collective-permute-done.1, bf16[512,1024]{1,0:T(8,128)(2,1)S(1)} %fusion.11, pred[512]{0:T(512)(128)(4,1)S(1)} %get-tuple-element.73, f32[1024]{0:T(1024)S(1)} %bitcast.99, ...), kind=kLoop, calls=%fused_computation.198 | loop fusion | flops 112720896 | bytes 3353600 | tf_op jit(solution)/shard_map/reduce_sum | solution.py:97
  122.6 18.7 %all-gather.5.cloned.1.call-done = bf16[1024,1024]{1,0:T(8,128)(2,1)} async-done(((bf16[1024,128]{1,0:T(8,128)(2,1)}), bf16[1024,1024]{1,0:T(8,128)(2,1)}) %all-gather.5.cloned.1.call-update) | async-done | bytes 2097168 | tf_op jit(solution)/shard_map/all_gather | solution.py:101
  141.3 0.0 copy-done.5
  141.3 0.0 copy-done.6
  141.3 4.1 %fusion.5 = bf16[512,1024]{1,0:T(8,128)(2,1)} fusion(bf16[512,1024]{1,0:T(8,128)(2,1)S(1)} %copy-done.2, bf16[1024,1024]{1,0:T(8,128)(2,1)} %all-gather.5.cloned.1.call-done, f32[512,1024]{1,0:T(8,128)S(1)} %get-tuple-element.8, f32[1024]{0:T(1024)S(1)} %copy-done.5, f32[1024]{0:T(1024)S(1)} %copy-done.6, f32[512]{0:T(512)S(1)} %get-tuple-element.75, ...), kind=kOutput, calls=%fused_computation.38 | convolution fusion | flops 1080557568 | bytes 6305792 | tf_op jit(solution)/shard_map/dot_general | solution.py:99
  (7 shorter events, 0.1 us)
Async XLA Ops:
  6.5 21.1 %copy-start = (s32[128]{0:T(128)S(1)}, s32[128]{0:T(128)}, u32[]{:S(2)}) copy-start(s32[128]{0:T(128)} %param.20) | copy-start | bytes 1540
  6.5 83.8 %all-gather.3.cloned.1.call-start = ((), (), s32[]{:S(2)}) async-start(), calls=%async_computation | async-start | bytes 4718592 | tf_op jit(solution)/shard_map/all_gather | solution.py:92
  17.0 124.3 %all-gather.5.cloned.1.call-start = ((), (), s32[]{:S(2)}) async-start(), calls=%async_computation.1 | async-start | bytes 2359296 | tf_op jit(solution)/shard_map/all_gather | solution.py:101
  27.6 3.8 %copy-start.1 = (s32[128]{0:T(128)S(1)}, s32[128]{0:T(128)}, u32[]{:S(2)}) copy-start(s32[128]{0:T(128)} %param.19) | copy-start | bytes 1540
  31.4 24.2 %copy-start.3 = (bf16[31,1024]{1,0:T(8,128)(2,1)S(1)}, bf16[31,1024]{1,0:T(8,128)(2,1)}, u32[]{:S(2)}) copy-start(bf16[31,1024]{1,0:T(8,128)(2,1)} %param.15) | copy-start | bytes 190468
  31.4 24.4 %copy-start.2 = (bf16[512,1024]{1,0:T(8,128)(2,1)S(1)}, bf16[512,1024]{1,0:T(8,128)(2,1)}, u32[]{:S(2)}) copy-start(bf16[512,1024]{1,0:T(8,128)(2,1)} %param.12) | copy-start | bytes 3145732
  90.3 3.6 %copy-start.4 = (f32[1024]{0:T(1024)S(1)}, f32[1024]{0:T(1024)}, u32[]{:S(2)}) copy-start(f32[1024]{0:T(1024)} %param.13) | copy-start | bytes 12292
  97.0 44.3 %copy-start.5 = (f32[1024]{0:T(1024)S(1)}, f32[1024]{0:T(1024)}, u32[]{:S(2)}) copy-start(f32[1024]{0:T(1024)} %param.17) | copy-start | bytes 12292
  97.1 44.3 %copy-start.6 = (f32[1024]{0:T(1024)S(1)}, f32[1024]{0:T(1024)}, u32[]{:S(2)}) copy-start(f32[1024]{0:T(1024)} %param.16) | copy-start | bytes 12292
  97.1 2.9 %collective-permute-start = (bf16[15,1024]{1,0:T(8,128)(2,1)S(1)}, bf16[15,1024]{1,0:T(8,128)(2,1)S(1)}, u32[]{:S(2)}, u32[]{:S(2)}) collective-permute-start(bf16[15,1024]{1,0:T(8,128)(2,1)S(1)} %get-tuple-element.11), channel_id=1, source_target_pairs={{0,1},{1,2},{2,3},{3,4},{4,5},{5,6},{6,7},{7,8},{8,9},{9,10},{10,1... | collective-permute-start | bytes 92168 | tf_op jit(solution)/shard_map/ppermute | solution.py:17
  98.4 4.9 %collective-permute-start.1 = (bf16[15,1024]{1,0:T(8,128)(2,1)S(1)}, bf16[15,1024]{1,0:T(8,128)(2,1)S(1)}, u32[]{:S(2)}, u32[]{:S(2)}) collective-permute-start(bf16[15,1024]{1,0:T(8,128)(2,1)S(1)} %get-tuple-element.12), channel_id=1, source_target_pairs={{1,0},{2,1},{3,2},{4,3},{5,4},{6,5},{7,6},{8,7},{9,8},{10,9},{11,1... | collective-permute-start | bytes 92168 | tf_op jit(solution)/shard_map/ppermute | solution.py:20
Sparse Core Ops, SparseCore 0:
  17.2 73.1 all-gather.2
  92.4 48.8 all-gather.4
where the time goes:
time: 153 us; the launch traced here: 152 us
  waiting for transfers between devices  55.8 us (36%)
  other arithmetic  41.3 us (27%)
  blocking collectives  17 us (11%)
  local copies, waits for them, and re-layouts  15.2 us (10%)
  between operations  13.6 us (9%)
  matrix products  6.55 us (4%)
  starting transfers between devices  2.81 us (2%)
    all_gather x1, waiting for transfers between devices, per_device(): lax.all_gather(w_in_rows, 'seq', axis=0, tiled=True)  33.8 us
    select_n x1, other arithmetic, frame_keys(): return (jnp.where(living, utterance, -1), living[margin:margin + row_count])  20.1 us
    reduce_sum x1, other arithmetic, per_device(): jnp.sum(mixed, axis=1)  19.4 us
    all_gather x1, waiting for transfers between devices, per_device(): lax.all_gather(w_out_rows, 'seq', axis=1, tiled=True)  18.7 us
    all_gather x1, blocking collectives, per_device(): lax.all_gather(w_in, 'grp', axis=2, tiled=True)  10.5 us
    all_gather x1, blocking collectives, per_device(): lax.all_gather(w_out, 'grp', axis=0, tiled=True)  6.53 us
    dot_general x1, matrix products, per_device(): jnp.dot(act, lax.all_gather(w_out_rows, 'seq', axis=1, tiled=True), prefe...  4.06 us
    gather x2, local copies, waits for them, and re-layouts, frame_keys(): living = inside & (position < jnp.take(lengths, utterance))  3.9 us
  transfers between devices with their start and end apart: 4, of which 3 were waited for; matrix products, arithmetic and copies ran while one was open for 39% of the time, Pallas kernels for 0%

commit v1 on v0

--- a/solution.py
+++ b/solution.py
@@ -85,7 +85,7 @@
     keys_wide, living = frame_keys(block_utt, block_off, lengths, own_first, row_count, margin)
     normed = layer_norm(frames, ln1_gain)
     w_in_rows, w_out_rows = (
-        lax.all_gather(w_in, "grp", axis=2, tiled=True),
+        jnp.concatenate(lax.all_gather(w_in, "grp"), axis=2),
         lax.all_gather(w_out, "grp", axis=0, tiled=True),
     )
     add_rows, empty = project_rows(normed, row_count, 2 * D)

time: 153 us -> 155 us (1.013)
  waiting for transfers between devices: 55.8 us -> 62.2 us
  local copies, waits for them, and re-layouts: 15.2 us -> 11 us
  matrix products: 6.55 us -> 8.67 us
  blocking collectives: 17 us -> 15 us
    all_gather x1, waiting for transfers between devices: 33.8 us -> 38.9 us  [per_device(): lax.all_gather(w_in_rows, 'seq', axis=0, tiled=True)]
    unnamed x15 -> x19, local copies, waits for them, and re-layouts: 3.67 us -> 1 us
    gather x2, local copies, waits for them, and re-layouts: 3.9 us -> 1.42 us  [frame_keys(): living = inside & (position < jnp.take(lengths, utterance))]
    dot_general x1, matrix products: 2.49 us -> 4.61 us  [add_rows(): jnp.dot(normed, weight_piece.reshape(piece_rows, -1), preferred_element_t...]
    all_gather x1, blocking collectives: 10.5 us -> 8.65 us  [per_device(): lax.all_gather(w_in, 'grp')]
  transfers between devices with their start and end apart: 4 -> 4, of which waited for: 3 -> 3; matrix products, arithmetic and copies ran while one was open for 39% -> 36% of each run, Pallas kernels for 0% -> 0%
where the time goes in v1:
time: 155 us; the launch traced here: 154 us
  waiting for transfers between devices  62.2 us (40%)
  other arithmetic  41.2 us (27%)
  blocking collectives  15 us (10%)
  between operations  13.6 us (9%)
  local copies, waits for them, and re-layouts  11 us (7%)
  matrix products  8.67 us (6%)
  starting transfers between devices  2.81 us (2%)
    all_gather x1, waiting for transfers between devices, per_device(): lax.all_gather(w_in_rows, 'seq', axis=0, tiled=True)  38.9 us
    select_n x1, other arithmetic, frame_keys(): return (jnp.where(living, utterance, -1), living[margin:margin + row_count])  20.1 us
    all_gather x1, waiting for transfers between devices, per_device(): lax.all_gather(w_out_rows, 'seq', axis=1, tiled=True)  19.9 us
    reduce_sum x1, other arithmetic, per_device(): jnp.sum(mixed, axis=1)  19.4 us
    all_gather x1, blocking collectives, per_device(): lax.all_gather(w_in, 'grp')  8.65 us
    all_gather x1, blocking collectives, per_device(): lax.all_gather(w_out, 'grp', axis=0, tiled=True)  6.3 us
    dot_general x1, matrix products, add_rows(): jnp.dot(normed, weight_piece.reshape(piece_rows, -1), preferred_element_t...  4.61 us
    dot_general x1, matrix products, per_device(): jnp.dot(act, lax.all_gather(w_out_rows, 'seq', axis=1, tiled=True), prefe...  4.06 us
  transfers between devices with their start and end apart: 4, of which 3 were waited for; matrix products, arithmetic and copies ran while one was open for 36% of the time, Pallas kernels for 0%

profile of v1, /device:TPU:0, one launch (start us, length us, event | category | flops | bytes accessed | tf_op | source)
XLA Modules:
  0.0 154.4 jit_solution(8378934198657159494)
XLA Ops:
  6.5 0.0 copy-start
  6.5 0.0 copy-start.5
  6.5 0.0 all-gather.4.cloned.1.call-start
  6.5 1.0 copy.11
  7.5 8.6 %all-gather = bf16[512,2,256]{2,0,1:T(8,128)(2,1)S(1)} all-gather(bf16[128,2,256]{2,0,1:T(8,128)(2,1)S(1)} %copy.11), channel_id=2, replica_groups=mesh['seq'=8,'grp'=4] {'grp'}, dimensions={0}, use_global_device_ids=true | all-gather | bytes 655360 | tf_op jit(solution)/shard_map/all_gather | solution.py:88
  16.2 1.0 copy.12
  17.1 0.0 all-gather.4.cloned.1.call-update
  17.2 0.0 all-gather.6.cloned.1.call-start
  17.2 0.0 copy-done.5
  17.2 6.3 %all_gather.18 = bf16[1024,128]{1,0:T(8,128)(2,1)} all-gather(bf16[256,128]{1,0:T(8,128)(2,1)S(1)} %copy-done.5), channel_id=1, replica_groups=mesh['seq'=8,'grp'=4] {'grp'}, dimensions={0}, use_global_device_ids=true | all-gather | bytes 327680 | tf_op jit(solution)/shard_map/all_gather | solution.py:89
  23.5 0.0 all-gather.6.cloned.1.call-update
  23.6 0.0 copy-done.3
  23.6 0.7 fusion.67
  24.3 0.7 fusion.68
  25.0 0.0 copy-done
  25.0 0.0 copy-start.1
  25.1 3.8 %gather_fusion = s32[542]{0:T(1024)S(1)} fusion(s32[128]{0:T(128)S(1)} %copy-done, s32[1024]{0:T(1024)S(1)} %pad_clamp_fusion), kind=kCustom, calls=%fused_computation.clone | custom fusion | bytes 6504 | tf_op jit(solution)/shard_map/jit(_take)/gather | solution.py:31
  28.9 0.0 copy-done.1
  28.9 0.0 copy-start.4
  28.9 0.0 copy-start.2
  28.9 3.8 %gather_fusion.1 = s32[542]{0:T(1024)S(1)} fusion(s32[128]{0:T(128)S(1)} %copy-done.1, s32[1024]{0:T(1024)S(1)} %pad_clamp_fusion), kind=kCustom, calls=%fused_computation.1.clone | custom fusion | bytes 6504 | tf_op jit(solution)/shard_map/jit(_take)/gather | solution.py:30
  32.7 0.0 copy-start.6
  32.7 20.1 %fusion.62 = (s32[542]{0:T(1024)S(1)}, pred[542]{0:T(1024)(128)(4,1)S(1)}) fusion(s32[542]{0:T(1024)S(1)} %gather_fusion.1, s32[]{:T(128)S(6)} %sub.32, s32[]{:T(128)} %bitcast.31, s32[]{:T(128)} %bitcast.30, s32[]{:T(128)} %bitcast.29, s32[]{:T(128)} %bitcast.28, s32[]{:T(128)} %bitcast.27, s32[]{:T(128)} %bitcast.26, s32[]{:T(128)} %bitcast.25, ...), kind=kLoop, calls=%fused_computation.161 | loop fusion | flops 57452 | bytes 7178 | tf_op jit(solution)/shard_map/jit(_where)/select_n | solution.py:33
  52.8 0.1 slice_compare_fusion.29
  52.9 0.1 slice_compare_fusion.28
  53.0 0.1 slice_compare_fusion.27
  53.0 0.0 copy-done.4
  53.1 0.1 slice_convert_fusion.30
  53.2 0.1 slice_convert_fusion.31
  53.2 0.0 copy-done.2
  53.2 0.2 convert_reduce_fusion
  53.5 0.4 fusion.2
  53.9 38.9 %all-gather.4.cloned.1.call-done = bf16[1024,2,1024]{0,2,1:T(8,128)(2,1)} async-done(((bf16[128,2,1024]{0,2,1:T(8,128)(2,1)}), bf16[1024,2,1024]{0,2,1:T(8,128)(2,1)}) %all-gather.4.cloned.1.call-update) | async-done | bytes 4194320 | tf_op jit(solution)/shard_map/all_gather | solution.py:92
  92.8 0.0 copy-done.6
  92.8 4.6 %fusion.12 = f32[512,2048]{1,0:T(8,128)S(1)} fusion(bf16[1024,2048]{0,1:T(8,128)(2,1)} %bitcast.103, bf16[512,1024]{1,0:T(8,128)(2,1)S(1)} %copy-done.2, f32[1024]{0:T(1024)S(1)} %copy-done.6, f32[512]{0:T(512)S(1)} %add_rsqrt_fusion.1, f32[512]{0:T(512)S(1)} %broadcast_multiply_fusion.1), kind=kOutput, calls=%fused_computation.49 | convolution fusion | flops 2150105088 | bytes 9445376 | tf_op jit(solution)/shard_map/dot_general | solution.py:72
  97.4 0.6 fusion.11
  98.0 0.0 copy-start.7
  98.0 0.0 copy-start.8
  98.0 1.3 collective-permute-start
  99.3 1.5 collective-permute-start.1
  100.8 0.1 slice_compare_fusion.26
  100.9 0.0 collective-permute-done
  100.9 3.3 %collective-permute-done.1 = bf16[15,1024]{1,0:T(8,128)(2,1)S(1)} collective-permute-done((bf16[15,1024]{1,0:T(8,128)(2,1)S(1)}, bf16[15,1024]{1,0:T(8,128)(2,1)S(1)}, u32[]{:S(2)}, u32[]{:S(2)}) %collective-permute-start.1) | collective-permute-done | bytes 30752 | tf_op jit(solution)/shard_map/ppermute | solution.py:20
  104.2 19.4 %fusion.64 = (f32[512]{0:T(512)S(1)}, f32[512]{0:T(512)S(1)}, f32[512,1024]{1,0:T(8,128)S(1)}) fusion(f32[1024]{0:T(1024)S(1)} %bitcast.101, bf16[15,1024]{1,0:T(8,128)(2,1)S(1)} %collective-permute-done.1, bf16[512,1024]{1,0:T(8,128)(2,1)S(1)} %fusion.11, pred[512]{0:T(512)(128)(4,1)S(1)} %get-tuple-element.73, f32[1024]{0:T(1024)S(1)} %bitcast.102, ...), kind=kLoop, calls=%fused_computation.198 | loop fusion | flops 112720896 | bytes 3353600 | tf_op jit(solution)/shard_map/reduce_sum | solution.py:97
  123.6 19.9 %all-gather.6.cloned.1.call-done = bf16[1024,1024]{1,0:T(8,128)(2,1)} async-done(((bf16[1024,128]{1,0:T(8,128)(2,1)}), bf16[1024,1024]{1,0:T(8,128)(2,1)}) %all-gather.6.cloned.1.call-update) | async-done | bytes 2097168 | tf_op jit(solution)/shard_map/all_gather | solution.py:101
  143.5 0.0 copy-done.7
  143.5 0.0 copy-done.8
  143.5 4.1 %fusion.5 = bf16[512,1024]{1,0:T(8,128)(2,1)} fusion(bf16[512,1024]{1,0:T(8,128)(2,1)S(1)} %copy-done.2, bf16[1024,1024]{1,0:T(8,128)(2,1)} %all-gather.6.cloned.1.call-done, f32[512,1024]{1,0:T(8,128)S(1)} %get-tuple-element.8, f32[1024]{0:T(1024)S(1)} %copy-done.7, f32[1024]{0:T(1024)S(1)} %copy-done.8, f32[512]{0:T(512)S(1)} %get-tuple-element.75, ...), kind=kOutput, calls=%fused_computation.38 | convolution fusion | flops 1080557568 | bytes 6305792 | tf_op jit(solution)/shard_map/dot_general | solution.py:99
  (8 shorter events, 0.1 us)
Async XLA Ops:
  6.5 18.5 %copy-start = (s32[128]{0:T(128)S(1)}, s32[128]{0:T(128)}, u32[]{:S(2)}) copy-start(s32[128]{0:T(128)} %param.20) | copy-start | bytes 1540
  6.5 10.7 %copy-start.5 = (bf16[256,128]{1,0:T(8,128)(2,1)S(1)}, bf16[256,128]{1,0:T(8,128)(2,1)}, u32[]{:S(2)}) copy-start(bf16[256,128]{1,0:T(8,128)(2,1)} %param.18) | copy-start | bytes 196612
  6.5 17.0 %copy-start.3 = (s32[32]{0:T(128)S(1)}, s32[32]{0:T(128)}, u32[]{:S(2)}) copy-start(s32[32]{0:T(128)} %param.21) | copy-start | bytes 388
  6.5 86.3 %all-gather.4.cloned.1.call-start = ((), (), s32[]{:S(2)}) async-start(), calls=%async_computation | async-start | bytes 4718592 | tf_op jit(solution)/shard_map/all_gather | solution.py:92
  17.2 126.4 %all-gather.6.cloned.1.call-start = ((), (), s32[]{:S(2)}) async-start(), calls=%async_computation.1 | async-start | bytes 2359296 | tf_op jit(solution)/shard_map/all_gather | solution.py:101
  25.0 3.8 %copy-start.1 = (s32[128]{0:T(128)S(1)}, s32[128]{0:T(128)}, u32[]{:S(2)}) copy-start(s32[128]{0:T(128)} %param.19) | copy-start | bytes 1540
  28.9 24.2 %copy-start.4 = (bf16[31,1024]{1,0:T(8,128)(2,1)S(1)}, bf16[31,1024]{1,0:T(8,128)(2,1)}, u32[]{:S(2)}) copy-start(bf16[31,1024]{1,0:T(8,128)(2,1)} %param.15) | copy-start | bytes 190468
  28.9 24.4 %copy-start.2 = (bf16[512,1024]{1,0:T(8,128)(2,1)S(1)}, bf16[512,1024]{1,0:T(8,128)(2,1)}, u32[]{:S(2)}) copy-start(bf16[512,1024]{1,0:T(8,128)(2,1)} %param.12) | copy-start | bytes 3145732
  32.7 60.1 %copy-start.6 = (f32[1024]{0:T(1024)S(1)}, f32[1024]{0:T(1024)}, u32[]{:S(2)}) copy-start(f32[1024]{0:T(1024)} %param.13) | copy-start | bytes 12292
  98.0 45.5 %copy-start.7 = (f32[1024]{0:T(1024)S(1)}, f32[1024]{0:T(1024)}, u32[]{:S(2)}) copy-start(f32[1024]{0:T(1024)} %param.17) | copy-start | bytes 12292
  98.0 45.5 %copy-start.8 = (f32[1024]{0:T(1024)S(1)}, f32[1024]{0:T(1024)}, u32[]{:S(2)}) copy-start(f32[1024]{0:T(1024)} %param.16) | copy-start | bytes 12292
  98.0 2.9 %collective-permute-start = (bf16[15,1024]{1,0:T(8,128)(2,1)S(1)}, bf16[15,1024]{1,0:T(8,128)(2,1)S(1)}, u32[]{:S(2)}, u32[]{:S(2)}) collective-permute-start(bf16[15,1024]{1,0:T(8,128)(2,1)S(1)} %get-tuple-element.11), channel_id=1, source_target_pairs={{0,1},{1,2},{2,3},{3,4},{4,5},{5,6},{6,7},{7,8},{8,9},{9,10},{10,1... | collective-permute-start | bytes 92168 | tf_op jit(solution)/shard_map/ppermute | solution.py:17
  99.3 4.9 %collective-permute-start.1 = (bf16[15,1024]{1,0:T(8,128)(2,1)S(1)}, bf16[15,1024]{1,0:T(8,128)(2,1)S(1)}, u32[]{:S(2)}, u32[]{:S(2)}) collective-permute-start(bf16[15,1024]{1,0:T(8,128)(2,1)S(1)} %get-tuple-element.12), channel_id=1, source_target_pairs={{1,0},{2,1},{3,2},{4,3},{5,4},{6,5},{7,6},{8,7},{9,8},{10,9},{11,1... | collective-permute-start | bytes 92168 | tf_op jit(solution)/shard_map/ppermute | solution.py:20
Sparse Core Ops, SparseCore 0:
  17.3 75.4 all-gather.3
  94.8 48.6 all-gather.5
